TPU v7x, 32 devices: a whole 2x2x4 slice. The times are simulated.
32 devices in a mesh: row: 4 (over z), col: 8 (over y, x, core).
Axes of the slice: x: 2, y: 2, z: 4, core: 2. Of those that a mesh axis runs over, the one named last changes fastest.
Arguments:
- latent: float32 [2, 1024, 2048], P(None, 'row', 'col'), may hold values from -3 to 3
- momentum: float32 [2, 1024, 2048], P(None, 'row', 'col'), may hold values from -4 to 4
- hyper_params: float32 [2, 2], replicated, may hold values from 0.3 to 0.7
- velocity: float32 [2, 2], replicated, may hold values from -3 to 3
- step_size: float32 [2], replicated, may hold values from 0.08 to 0.12
- counts: int32 [1024, 2048], P('row', 'col'), may hold values from 0 to 7
- kappa_field: float32 [1024, 2048], P('row', 'col'), may hold values from 0.1 to 1
Outputs:
- latent_out: float32 [2, 1024, 2048], P(None, 'row', 'col')
- momentum_out: float32 [2, 1024, 2048], P(None, 'row', 'col')
- hyper_out: float32 [2, 2], replicated
- velocity_out: float32 [2, 2], replicated
All inputs are finite; a program needn't handle non-finite values.
Results may differ from a plain program's by a relative error of at most 0.0001.
Values sent between devices are 32-bit elements; how exact they have to be, the bound alone decides.
A program may use at most 64 MiB of HBM per device.

v0:
```python
import jax
import jax.numpy as jnp
from jax import lax
from jax.sharding import PartitionSpec as P

STEPS = 10


def padded(cells, sides, width):
    for axis, dim in sides:
        count = lax.axis_size(axis)
        head = lax.slice_in_dim(cells, 0, width, axis=dim)
        tail = lax.slice_in_dim(cells, cells.shape[dim] - width, cells.shape[dim], axis=dim)
        cells = jnp.concatenate(
            [
                lax.ppermute(tail, axis, [(i, (i + 1) % count) for i in range(count)]),
                cells,
                lax.ppermute(head, axis, [((i + 1) % count, i) for i in range(count)]),
            ],
            axis=dim,
        )
    return cells


def local_gradient(widened, count_part, kappa_part, offset, tau_value, margin):
    center = widened[:, 1:-1, 1:-1]
    beside = (
        widened[:, :-2, 1:-1] + widened[:, 2:, 1:-1] + widened[:, 1:-1, :-2] + widened[:, 1:-1, 2:]
    )
    applied = (kappa_part + 4.0) * center - beside
    intensity = jnp.exp(offset[:, None, None] + center)
    gradient = tau_value[:, None, None] * applied - count_part + intensity
    weighted = center * applied
    excess_terms = intensity - count_part
    if margin:
        weighted = weighted[:, margin:-margin, margin:-margin]
        excess_terms = excess_terms[:, margin:-margin, margin:-margin]
    return (gradient, jnp.sum(weighted, axis=(1, 2)), jnp.sum(excess_terms, axis=(1, 2)))


def acceleration(quadratic, excess, tau_value, total):
    stacked = jnp.stack([quadratic, excess])
    summed = lax.psum(stacked, ("row", "col"))
    return jnp.stack([summed[1] / total, 0.5 * tau_value * summed[0] / total - 0.5])


def trimmed(array, layers):
    return array[..., layers:-layers, layers:-layers]


def shards(latent, momentum, hyper_params, velocity, step_size, counts, kappa_field):
    count_float = counts.astype(jnp.float32)
    total = float(latent.shape[1] * latent.shape[2] * lax.axis_size("row") * lax.axis_size("col"))
    size_grid = step_size[:, None, None]
    layers_deep = 5
    wide_counts, wide_kappa = (
        padded(count_float, (("row", 0), ("col", 1)), layers_deep),
        padded(kappa_field, (("row", 0), ("col", 1)), layers_deep),
    )
    field, moment, params, speed = (latent, momentum, hyper_params, velocity)
    accel = jnp.zeros_like(velocity)
    for index_block in range(STEPS // layers_deep):
        field, moment = (
            padded(field, (("row", 1), ("col", 2)), layers_deep + 1),
            padded(moment, (("row", 1), ("col", 2)), layers_deep + 1),
        )
        moment = trimmed(moment, 1)
        tau_value = jnp.exp(params[1])
        gradient, quadratic, excess = local_gradient(
            field, wide_counts, wide_kappa, params[0], tau_value, layers_deep
        )
        if index_block == 0:
            accel = acceleration(quadratic, excess, tau_value, total)
        for inner in range(layers_deep):
            width_now = layers_deep - inner
            field = trimmed(field, 1)
            moment = moment - 0.5 * size_grid * gradient
            speed = speed - 0.5 * step_size * accel
            field = field + size_grid * moment
            params = params + step_size * speed
            tau_value = jnp.exp(params[1])
            gradient, quadratic, excess = local_gradient(
                field,
                trimmed(wide_counts, inner + 1),
                trimmed(wide_kappa, inner + 1),
                params[0],
                tau_value,
                width_now - 1,
            )
            accel = acceleration(quadratic, excess, tau_value, total)
            moment = trimmed(moment, 1) - 0.5 * size_grid * gradient
            speed = speed - 0.5 * step_size * accel
        field = trimmed(field, 1)
    return (field, moment, params, speed)


def solution(mesh):
    placed = (
        P(None, "row", "col"),
        P(None, "row", "col"),
        P(),
        P(),
        P(),
        P("row", "col"),
        P("row", "col"),
    )
    return jax.shard_map(
        shards,
        mesh=mesh,
        in_specs=placed,
        out_specs=(P(None, "row", "col"), P(None, "row", "col"), P(), P()),
        check_vma=False,
    )
```

profile of v0, /device:TPU:0, one launch (start us, length us, event | category | flops | bytes accessed | tf_op | source)
XLA Modules:
  0.0 555.2 jit_solution(2762371303259821550)
XLA Ops:
  0.6 0.7 fusion.69
  1.4 5.1 collective-permute-start.1
  6.5 1.0 convert_element_type.3
  7.5 3.8 collective-permute-start.13
  11.4 2.0 collective-permute-start.8
  13.4 0.8 fusion.68
  14.2 0.8 collective-permute-done.9
  15.0 1.9 collective-permute-done.8
  16.9 1.9 collective-permute-start.5
  19.1 1.4 collective-permute-done.12
  20.6 1.0 collective-permute-done.11
  21.7 2.8 collective-permute-start.15
  24.4 1.6 collective-permute-done.10
  26.3 0.9 slice_add_fusion.39
  27.2 0.9 slice_add_fusion.38
  28.1 0.9 slice_add_fusion.37
  29.3 2.1 collective-permute-done.14
  32.0 1.1 collective-permute-start.3
  33.1 1.7 collective-permute-done.4
  35.0 1.5 collective-permute-start.7
  36.5 3.6 collective-permute-done.3
  40.2 2.8 collective-permute-done.2
  43.4 1.7 collective-permute-done.7
  45.1 2.0 collective-permute-done.6
  47.1 2.3 multiply_add_fusion.1
  49.4 0.6 fusion.34
  50.0 0.9 slice.714
  50.9 38.5 %psum.77 = f32[2,2]{1,0:T(2,128)S(1)} all-reduce(f32[2,2]{1,0:T(2,128)S(1)} %pad_maximum_fusion.18), channel_id=1, replica_groups=mesh['row'=4,'col'=8] {'row','col'}, use_global_device_ids=true, to_apply=%region_2.0 | all-reduce | flops 4 | bytes 32 | tf_op jit(solution)/shard_map/psum | solution.py:43
  89.4 0.7 copy-done.17
  90.1 3.4 multiply_add_fusion.9
  94.3 0.9 slice.726
  95.2 40.3 %psum.78 = f32[2,2]{1,0:T(2,128)S(1)} all-reduce(f32[2,2]{1,0:T(2,128)S(1)} %pad_maximum_fusion.19), channel_id=1, replica_groups=mesh['row'=4,'col'=8] {'row','col'}, use_global_device_ids=true, to_apply=%region_5.0 | all-reduce | flops 4 | bytes 32 | tf_op jit(solution)/shard_map/psum | solution.py:43
  135.6 3.4 multiply_add_fusion.8
  139.8 0.9 slice.738
  140.7 39.6 %psum.79 = f32[2,2]{1,0:T(2,128)S(1)} all-reduce(f32[2,2]{1,0:T(2,128)S(1)} %pad_maximum_fusion.20), channel_id=1, replica_groups=mesh['row'=4,'col'=8] {'row','col'}, use_global_device_ids=true, to_apply=%region_8.0 | all-reduce | flops 4 | bytes 32 | tf_op jit(solution)/shard_map/psum | solution.py:43
  180.4 3.4 multiply_add_fusion.7
  184.6 0.9 slice.750
  185.5 40.3 %psum.80 = f32[2,2]{1,0:T(2,128)S(1)} all-reduce(f32[2,2]{1,0:T(2,128)S(1)} %pad_maximum_fusion.21), channel_id=1, replica_groups=mesh['row'=4,'col'=8] {'row','col'}, use_global_device_ids=true, to_apply=%region_11.0 | all-reduce | flops 4 | bytes 32 | tf_op jit(solution)/shard_map/psum | solution.py:43
  225.9 3.4 multiply_add_fusion.6
  230.6 39.5 %psum.81 = f32[2,2]{1,0:T(2,128)S(1)} all-reduce(f32[2,2]{1,0:T(2,128)S(1)} %pad_maximum_fusion.22), channel_id=1, replica_groups=mesh['row'=4,'col'=8] {'row','col'}, use_global_device_ids=true, to_apply=%region_14.0 | all-reduce | flops 4 | bytes 32 | tf_op jit(solution)/shard_map/psum | solution.py:43
  270.1 0.7 multiply_reduce_fusion.1
  270.9 40.5 %psum.82 = f32[2,2]{1,0:T(2,128)S(1)} all-reduce(f32[2,2]{1,0:T(2,128)S(1)} %pad_maximum_fusion.23), channel_id=1, replica_groups=mesh['row'=4,'col'=8] {'row','col'}, use_global_device_ids=true, to_apply=%region_17.0 | all-reduce | flops 4 | bytes 32 | tf_op jit(solution)/shard_map/psum | solution.py:43
  311.4 2.2 collective-permute-start.17
  313.5 1.5 slice_subtract_fusion.6
  315.1 3.9 collective-permute-start.21
  319.8 0.6 collective-permute-done.21
  320.4 4.1 collective-permute-done.20
  324.7 0.5 collective-permute-start.22
  325.2 4.5 collective-permute-done.18
  330.1 0.8 collective-permute-done.23
  330.9 4.7 collective-permute-done.22
  335.7 1.3 multiply_add_fusion
  337.0 2.1 multiply_add_fusion.5
  339.9 39.1 %psum.83 = f32[2,2]{1,0:T(2,128)S(1)} all-reduce(f32[2,2]{1,0:T(2,128)S(1)} %pad_maximum_fusion.24), channel_id=1, replica_groups=mesh['row'=4,'col'=8] {'row','col'}, use_global_device_ids=true, to_apply=%region_20.0 | all-reduce | flops 4 | bytes 32 | tf_op jit(solution)/shard_map/psum | solution.py:43
  379.0 3.2 multiply_add_fusion.4
  383.0 40.9 %psum.84 = f32[2,2]{1,0:T(2,128)S(1)} all-reduce(f32[2,2]{1,0:T(2,128)S(1)} %pad_maximum_fusion.25), channel_id=1, replica_groups=mesh['row'=4,'col'=8] {'row','col'}, use_global_device_ids=true, to_apply=%region_23.0 | all-reduce | flops 4 | bytes 32 | tf_op jit(solution)/shard_map/psum | solution.py:43
  424.0 3.2 multiply_add_fusion.3
  427.9 39.1 %psum.85 = f32[2,2]{1,0:T(2,128)S(1)} all-reduce(f32[2,2]{1,0:T(2,128)S(1)} %pad_maximum_fusion.26), channel_id=1, replica_groups=mesh['row'=4,'col'=8] {'row','col'}, use_global_device_ids=true, to_apply=%region_26.0 | all-reduce | flops 4 | bytes 32 | tf_op jit(solution)/shard_map/psum | solution.py:43
  467.1 3.2 multiply_add_fusion.2
  471.0 40.9 %psum.86 = f32[2,2]{1,0:T(2,128)S(1)} all-reduce(f32[2,2]{1,0:T(2,128)S(1)} %pad_maximum_fusion.27), channel_id=1, replica_groups=mesh['row'=4,'col'=8] {'row','col'}, use_global_device_ids=true, to_apply=%region_29.0 | all-reduce | flops 4 | bytes 32 | tf_op jit(solution)/shard_map/psum | solution.py:43
  512.0 1.4 multiply_reduce_fusion
  513.4 39.1 %psum.87 = f32[2,2]{1,0:T(2,128)S(1)} all-reduce(f32[2,2]{1,0:T(2,128)S(1)} %pad_maximum_fusion.28), channel_id=1, replica_groups=mesh['row'=4,'col'=8] {'row','col'}, use_global_device_ids=true, to_apply=%region_32.0 | all-reduce | flops 4 | bytes 32 | tf_op jit(solution)/shard_map/psum | solution.py:43
  552.5 0.6 fusion.37
  553.1 2.1 slice_subtract_fusion.1
  (142 shorter events, 10.6 us)
Async XLA Ops:
  1.4 30.4 %collective-permute-start.1 = (f32[2,6,256]{2,1,0:T(8,128)S(1)}, f32[2,6,256]{2,1,0:T(8,128)S(1)}, u32[]{:S(2)}, u32[]{:S(2)}) collective-permute-start(f32[2,6,256]{2,1,0:T(8,128)S(1)} %get-tuple-element.87), channel_id=1, source_target_pairs={{8,0},{16,8},{24,16},{0,24},{9,1},{17,9},{25,17},{1,25},{10,2},{18... | collective-permute-start | bytes 36872 | tf_op jit(solution)/shard_map/ppermute | solution.py:18
  6.5 4.9 copy-start.7
  6.5 25.3 %collective-permute-start = (f32[2,6,256]{2,1,0:T(8,128)S(1)}, f32[2,6,256]{2,1,0:T(8,128)S(1)}, u32[]{:S(2)}, u32[]{:S(2)}) collective-permute-start(f32[2,6,256]{2,1,0:T(8,128)S(1)} %get-tuple-element.86), channel_id=1, source_target_pairs={{0,8},{8,16},{16,24},{24,0},{1,9},{9,17},{17,25},{25,1},{2,10},{10... | collective-permute-start | bytes 36872 | tf_op jit(solution)/shard_map/ppermute | solution.py:16
  7.5 11.5 %collective-permute-start.13 = (f32[5,256]{1,0:T(8,128)S(1)}, f32[5,256]{1,0:T(8,128)S(1)}, u32[]{:S(2)}, u32[]{:S(2)}) collective-permute-start(f32[5,256]{1,0:T(8,128)S(1)} %get-tuple-element.95), channel_id=1, source_target_pairs={{8,0},{16,8},{24,16},{0,24},{9,1},{17,9},{25,17},{1,25},{10,2},{18... | collective-permute-start | bytes 15368 | tf_op jit(solution)/shard_map/ppermute | solution.py:18
  11.3 2.1 copy-start.16
  11.3 3.7 collective-permute-start.9
  11.4 5.5 collective-permute-start.8
  13.4 0.8 copy-start.15
  15.0 5.4 collective-permute-start.12
  16.9 16.2 %collective-permute-start.5 = (f32[2,6,256]{2,1,0:T(8,128)S(1)}, f32[2,6,256]{2,1,0:T(8,128)S(1)}, u32[]{:S(2)}, u32[]{:S(2)}) collective-permute-start(f32[2,6,256]{2,1,0:T(8,128)S(1)} %get-tuple-element.85), channel_id=1, source_target_pairs={{8,0},{16,8},{24,16},{0,24},{9,1},{17,9},{25,17},{1,25},{10,2},{18... | collective-permute-start | bytes 36872 | tf_op jit(solution)/shard_map/ppermute | solution.py:18
  19.0 2.7 collective-permute-start.11
  20.5 5.5 collective-permute-start.10
  21.7 7.5 %collective-permute-start.15 = (f32[266,5]{1,0:T(8,128)S(1)}, f32[266,5]{1,0:T(8,128)S(1)}, u32[]{:S(2)}, u32[]{:S(2)}) collective-permute-start(f32[266,5]{1,0:T(8,128)S(1)} %get-tuple-element.91), channel_id=1, source_target_pairs={{1,0},{2,1},{3,2},{4,3},{5,4},{6,5},{7,6},{0,7},{9,8},{10,9},{11,1... | collective-permute-start | bytes 15968 | tf_op jit(solution)/shard_map/ppermute | solution.py:18
  26.0 5.4 collective-permute-start.14
  29.2 2.6 copy-start.12
  29.2 5.6 %collective-permute-start.4 = (f32[2,6,256]{2,1,0:T(8,128)S(1)}, f32[2,6,256]{2,1,0:T(8,128)S(1)}, u32[]{:S(2)}, u32[]{:S(2)}) collective-permute-start(f32[2,6,256]{2,1,0:T(8,128)S(1)} %get-tuple-element.84), channel_id=1, source_target_pairs={{0,8},{8,16},{16,24},{24,0},{1,9},{9,17},{17,25},{25,1},{2,10},{10... | collective-permute-start | bytes 36872 | tf_op jit(solution)/shard_map/ppermute | solution.py:16
  31.9 3.0 copy-start.11
  32.0 8.2 %collective-permute-start.3 = (f32[2,268,6]{2,1,0:T(8,128)S(1)}, f32[2,268,6]{2,1,0:T(8,128)S(1)}, u32[]{:S(2)}, u32[]{:S(2)}) collective-permute-start(f32[2,268,6]{2,1,0:T(8,128)S(1)} %get-tuple-element.81), channel_id=1, source_target_pairs={{1,0},{2,1},{3,2},{4,3},{5,4},{6,5},{7,6},{0,7},{9,8},{10,9},{11,1... | collective-permute-start | bytes 38600 | tf_op jit(solution)/shard_map/ppermute | solution.py:18
  33.1 9.9 %collective-permute-start.2 = (f32[2,268,6]{2,1,0:T(8,128)S(1)}, f32[2,268,6]{2,1,0:T(8,128)S(1)}, u32[]{:S(2)}, u32[]{:S(2)}) collective-permute-start(f32[2,268,6]{2,1,0:T(8,128)S(1)} %get-tuple-element.80), channel_id=1, source_target_pairs={{0,1},{1,2},{2,3},{3,4},{4,5},{5,6},{6,7},{7,0},{8,9},{9,10},{10,1... | collective-permute-start | bytes 38600 | tf_op jit(solution)/shard_map/ppermute | solution.py:16
  35.0 10.1 %collective-permute-start.7 = (f32[2,268,6]{2,1,0:T(8,128)S(1)}, f32[2,268,6]{2,1,0:T(8,128)S(1)}, u32[]{:S(2)}, u32[]{:S(2)}) collective-permute-start(f32[2,268,6]{2,1,0:T(8,128)S(1)} %get-tuple-element.79), channel_id=1, source_target_pairs={{1,0},{2,1},{3,2},{4,3},{5,4},{6,5},{7,6},{0,7},{9,8},{10,9},{11,1... | collective-permute-start | bytes 38600 | tf_op jit(solution)/shard_map/ppermute | solution.py:18
  36.5 10.6 %collective-permute-start.6 = (f32[2,268,6]{2,1,0:T(8,128)S(1)}, f32[2,268,6]{2,1,0:T(8,128)S(1)}, u32[]{:S(2)}, u32[]{:S(2)}) collective-permute-start(f32[2,268,6]{2,1,0:T(8,128)S(1)} %get-tuple-element.78), channel_id=1, source_target_pairs={{0,1},{1,2},{2,3},{3,4},{4,5},{5,6},{6,7},{7,0},{8,9},{9,10},{10,1... | collective-permute-start | bytes 38600 | tf_op jit(solution)/shard_map/ppermute | solution.py:16
  89.4 0.7 copy-start.17
  229.6 0.9 copy-start.8
  230.5 40.3 %copy-start.9 = (f32[256,256]{1,0:T(8,128)}, f32[256,256]{1,0:T(8,128)S(1)}, u32[]{:S(2)}) copy-start(f32[256,256]{1,0:T(8,128)S(1)} %broadcast_add_fusion.1) | copy-start | bytes 786436
  311.4 7.6 %collective-permute-start.17 = (f32[2,6,256]{2,1,0:T(8,128)S(1)}, f32[2,6,256]{2,1,0:T(8,128)S(1)}, u32[]{:S(2)}, u32[]{:S(2)}) collective-permute-start(f32[2,6,256]{2,1,0:T(8,128)S(1)} %get-tuple-element.70), channel_id=1, source_target_pairs={{8,0},{16,8},{24,16},{0,24},{9,1},{17,9},{25,17},{1,25},{10,2},{18... | collective-permute-start | bytes 36872 | tf_op jit(solution)/shard_map/ppermute | solution.py:18
  313.5 5.5 collective-permute-start.16
  315.1 5.3 collective-permute-start.21
  319.0 5.5 collective-permute-start.20
  319.3 6.0 %collective-permute-start.19 = (f32[2,268,6]{2,1,0:T(8,128)S(1)}, f32[2,268,6]{2,1,0:T(8,128)S(1)}, u32[]{:S(2)}, u32[]{:S(2)}) collective-permute-start(f32[2,268,6]{2,1,0:T(8,128)S(1)} %get-tuple-element.77), channel_id=1, source_target_pairs={{1,0},{2,1},{3,2},{4,3},{5,4},{6,5},{7,6},{0,7},{9,8},{10,9},{11,1... | collective-permute-start | bytes 38600 | tf_op jit(solution)/shard_map/ppermute | solution.py:18
  319.3 10.4 %collective-permute-start.18 = (f32[2,268,6]{2,1,0:T(8,128)S(1)}, f32[2,268,6]{2,1,0:T(8,128)S(1)}, u32[]{:S(2)}, u32[]{:S(2)}) collective-permute-start(f32[2,268,6]{2,1,0:T(8,128)S(1)} %get-tuple-element.76), channel_id=1, source_target_pairs={{0,1},{1,2},{2,3},{3,4},{4,5},{5,6},{6,7},{7,0},{8,9},{9,10},{10,1... | collective-permute-start | bytes 38600 | tf_op jit(solution)/shard_map/ppermute | solution.py:16
  324.7 6.2 %collective-permute-start.23 = (f32[2,268,6]{2,1,0:T(8,128)S(1)}, f32[2,268,6]{2,1,0:T(8,128)S(1)}, u32[]{:S(2)}, u32[]{:S(2)}) collective-permute-start(f32[2,268,6]{2,1,0:T(8,128)S(1)} %get-tuple-element.75), channel_id=1, source_target_pairs={{1,0},{2,1},{3,2},{4,3},{5,4},{6,5},{7,6},{0,7},{9,8},{10,9},{11,1... | collective-permute-start | bytes 38600 | tf_op jit(solution)/shard_map/ppermute | solution.py:18
  324.7 10.9 %collective-permute-start.22 = (f32[2,268,6]{2,1,0:T(8,128)S(1)}, f32[2,268,6]{2,1,0:T(8,128)S(1)}, u32[]{:S(2)}, u32[]{:S(2)}) collective-permute-start(f32[2,268,6]{2,1,0:T(8,128)S(1)} %get-tuple-element.74), channel_id=1, source_target_pairs={{0,1},{1,2},{2,3},{3,4},{4,5},{5,6},{6,7},{7,0},{8,9},{9,10},{10,1... | collective-permute-start | bytes 38600 | tf_op jit(solution)/shard_map/ppermute | solution.py:16
  330.1 6.9 %copy-start.2 = (f32[264,264]{1,0:T(8,128)S(1)}, f32[264,264]{1,0:T(8,128)}, u32[]{:S(2)}) copy-start(f32[264,264]{1,0:T(8,128)} %slice_add_fusion.39) | copy-start | bytes 836356
  330.1 6.9 %copy-start.6 = (f32[264,264]{1,0:T(8,128)S(1)}, f32[264,264]{1,0:T(8,128)}, u32[]{:S(2)}) copy-start(f32[264,264]{1,0:T(8,128)} %slice.714) | copy-start | bytes 836356
  339.4 39.6 %copy-start.1 = (f32[262,262]{1,0:T(8,128)S(1)}, f32[262,262]{1,0:T(8,128)}, u32[]{:S(2)}) copy-start(f32[262,262]{1,0:T(8,128)} %slice_add_fusion.38) | copy-start | bytes 823732
  339.4 39.6 %copy-start.5 = (f32[262,262]{1,0:T(8,128)S(1)}, f32[262,262]{1,0:T(8,128)}, u32[]{:S(2)}) copy-start(f32[262,262]{1,0:T(8,128)} %slice.726) | copy-start | bytes 823732
  382.5 41.4 %copy-start = (f32[260,260]{1,0:T(8,128)S(1)}, f32[260,260]{1,0:T(8,128)}, u32[]{:S(2)}) copy-start(f32[260,260]{1,0:T(8,128)} %slice_add_fusion.37) | copy-start | bytes 811204
  382.5 41.5 %copy-start.4 = (f32[260,260]{1,0:T(8,128)S(1)}, f32[260,260]{1,0:T(8,128)}, u32[]{:S(2)}) copy-start(f32[260,260]{1,0:T(8,128)} %slice.738) | copy-start | bytes 811204
  427.5 39.6 %copy-start.3 = (f32[258,258]{1,0:T(8,128)S(1)}, f32[258,258]{1,0:T(8,128)}, u32[]{:S(2)}) copy-start(f32[258,258]{1,0:T(8,128)} %slice.750) | copy-start | bytes 798772
  470.6 41.4 %copy-start.10 = (f32[256,256]{1,0:T(8,128)S(1)}, f32[256,256]{1,0:T(8,128)}, u32[]{:S(2)}) copy-start(f32[256,256]{1,0:T(8,128)} %copy-done.9) | copy-start | bytes 786436
  511.9 40.6 %copy-start.18 = (f32[2,2]{1,0:T(2,128)}, f32[2,2]{1,0:T(2,128)S(1)}, u32[]{:S(2)}) copy-start(f32[2,2]{1,0:T(2,128)S(1)} %get-tuple-element.10) | copy-start | bytes 52
  511.9 41.1 %copy-start.13 = (f32[2,258,258]{2,1,0:T(8,128)S(1)}, f32[2,258,258]{2,1,0:T(8,128)}, u32[]{:S(2)}) copy-start(f32[2,258,258]{2,1,0:T(8,128)} %get-tuple-element.13) | copy-start | bytes 1597540
  513.4 41.8 %copy-start.14 = (f32[2,256,256]{2,1,0:T(8,128)}, f32[2,256,256]{2,1,0:T(8,128)S(1)}, u32[]{:S(2)}) copy-start(f32[2,256,256]{2,1,0:T(8,128)S(1)} %get-tuple-element.9) | copy-start | bytes 1572868
where the time goes:
time: 557 us; the launch traced here: 555 us
  blocking collectives  438 us (79%)
  other arithmetic  47.7 us (9%)
  waiting for transfers between devices  35.5 us (6%)
  starting transfers between devices  25.7 us (5%)
  local copies, waits for them, and re-layouts  7.47 us (1%)
    psum x11, blocking collectives, acceleration(): summed = lax.psum(stacked, ('row', 'col'))  438 us
    add x10, other arithmetic, shards(): field = field + size_grid * moment  29 us
    ppermute x12, waiting for transfers between devices, padded(): lax.ppermute(tail, axis, [(i, (i + 1) % count) for i in range(count)])  26.8 us
    ppermute x12, starting transfers between devices, padded(): lax.ppermute(head, axis, [((i + 1) % count, i) for i in range(count)])  22.6 us
  transfers between devices with their start and end apart: 24, of which 17 were waited for; matrix products, arithmetic and copies ran while one was open for 2% of the time, Pallas kernels for 0%

commit v1 on v0

v1 whole, which is shorter than its diff:
```python
import functools

import jax
import jax.numpy as jnp
from jax import lax
from jax.experimental import pallas as pl
from jax.experimental.pallas import tpu as pltpu
from jax.sharding import PartitionSpec as P

STEPS = 10
HALO = 16
PAD = 8
TOP = PAD + HALO
LANES = 128
SEG = 16
MESH = pl.DeviceIdType.MESH


def kernel(
    sizes, latent, momentum, counts, kappa, hyper, velocity, step_size,
    latent_out, momentum_out, hyper_out, velocity_out,
    state, applied, intensity, raw_counts, left_pack, right_pack, from_right, from_left,
    payload, gathered,
    load_sem, store_sem, halo_send, halo_recv, sum_send, sum_recv,
):
    nr, nc, chains, rows, tiles, total = sizes
    devices = nr * nc
    row, col = lax.axis_index("row"), lax.axis_index("col")
    me = row * nc + col
    arrays = 2 * chains + 2
    kap, cnt = 2 * chains, 2 * chains + 1
    own = pl.ds(TOP, rows)

    loads = []
    for c in range(chains):
        for j in range(tiles):
            cols = pl.ds(j * LANES, LANES)
            loads.append((latent.at[c, :, cols], state.at[c, j, own, :]))
            loads.append((momentum.at[c, :, cols], state.at[chains + c, j, own, :]))
    for j in range(tiles):
        cols = pl.ds(j * LANES, LANES)
        loads.append((kappa.at[:, cols], state.at[kap, j, own, :]))
        loads.append((counts.at[:, cols], raw_counts.at[j]))
    loads = [pltpu.make_async_copy(s, d, load_sem.at[i]) for i, (s, d) in enumerate(loads)]
    for copy in loads:
        copy.start()

    def peer(d):
        other = lax.rem(me + d, devices)
        return (other // nc, lax.rem(other, nc))

    barrier = pltpu.get_barrier_semaphore()
    for d in range(1, devices):
        pl.semaphore_signal(barrier, inc=1, device_id=peer(d), device_id_type=MESH)

    lane = lax.broadcasted_iota(jnp.int32, (8, LANES), 1)
    seg = lane // SEG
    sublane = lax.broadcasted_iota(jnp.int32, (8, LANES), 0)
    first, last = lane == 0, lane == LANES - 1

    for copy in loads:
        copy.wait()

    def pack(i, counted):
        rel = pl.multiple_of(i * 8, 8)
        r = pl.multiple_of(TOP + i * 8, 8)
        for j in range(tiles):
            value = raw_counts[j, pl.ds(rel, 8), :].astype(jnp.float32)
            state[cnt, j, pl.ds(r, 8), :] = value
            counted = counted + value
        lp = state[0, 0, pl.ds(r, 8), :]
        rp = pltpu.roll(state[0, tiles - 1, pl.ds(r, 8), :], SEG, 1)
        for a in range(1, arrays):
            lp = jnp.where(seg == a, pltpu.roll(state[a, 0, pl.ds(r, 8), :], SEG * a, 1), lp)
            rolled = pltpu.roll(state[a, tiles - 1, pl.ds(r, 8), :], SEG * (a + 1) % LANES, 1)
            rp = jnp.where(seg == a, rolled, rp)
        left_pack[pl.ds(rel, 8), :] = lp
        right_pack[pl.ds(rel, 8), :] = rp
        return counted

    counted = lax.fori_loop(0, rows // 8, pack, jnp.zeros((8, LANES), jnp.float32))

    pl.semaphore_wait(barrier, devices - 1)

    up, down = lax.rem(row + nr - 1, nr), lax.rem(row + 1, nr)
    left, right = lax.rem(col + nc - 1, nc), lax.rem(col + 1, nc)
    head, tail = pl.ds(0, HALO), pl.ds(rows - HALO, HALO)
    body, below = pl.ds(HALO, rows), pl.ds(HALO + rows, HALO)
    halos = [
        (left_pack.at[:, :], from_right.at[body, :], (row, left)),
        (right_pack.at[:, :], from_left.at[body, :], (row, right)),
        (
            state.at[:, pl.ds(0, tiles), pl.ds(TOP, HALO), :],
            state.at[:, pl.ds(0, tiles), pl.ds(TOP + rows, HALO), :],
            (up, col),
        ),
        (
            state.at[:, pl.ds(0, tiles), pl.ds(TOP + rows - HALO, HALO), :],
            state.at[:, pl.ds(0, tiles), pl.ds(PAD, HALO), :],
            (down, col),
        ),
        (left_pack.at[tail, :], from_right.at[head, :], (down, left)),
        (left_pack.at[head, :], from_right.at[below, :], (up, left)),
        (right_pack.at[tail, :], from_left.at[head, :], (down, right)),
        (right_pack.at[head, :], from_left.at[below, :], (up, right)),
    ]
    halos = [
        pltpu.make_async_remote_copy(
            src_ref=s, dst_ref=d, send_sem=halo_send.at[i], recv_sem=halo_recv.at[i],
            device_id=where, device_id_type=MESH,
        )
        for i, (s, d, where) in enumerate(halos)
    ]
    for copy in halos:
        copy.start()
    for copy in halos:
        copy.wait()

    def unpack(i, carry):
        rel = pl.multiple_of(i * 8, 8)
        r = pl.multiple_of(PAD + i * 8, 8)
        fr = from_right[pl.ds(rel, 8), :]
        fl = from_left[pl.ds(rel, 8), :]
        for a in range(arrays):
            right_part = pltpu.roll(fr, (LANES - SEG * a) % LANES, 1)
            left_part = pltpu.roll(fl, (LANES - SEG * (a + 1)) % LANES, 1)
            value = jnp.where(seg == 0, right_part, jnp.where(seg == 7, left_part, 0.0))
            state[a, tiles, pl.ds(r, 8), :] = value
        return carry

    lax.fori_loop(0, (rows + 2 * HALO) // 8, unpack, 0)

    def stencil_tiles(r, lane_tiles):
        rowset = pl.ds(r, 8)
        terms = []
        for c in range(chains):
            full = [state[c, j, rowset, :] for j in range(tiles + 1)]
            to_right = [pltpu.roll(x, 1, 1) for x in full]
            to_left = [pltpu.roll(x, LANES - 1, 1) for x in full]
            quad = mass = None
            for j in lane_tiles:
                v = full[j]
                beside = jnp.where(first, to_right[j - 1], to_right[j])
                beside += jnp.where(last, to_left[(j + 1) % (tiles + 1)], to_left[j])
                beside += state[c, j, pl.ds(r - 1, 8), :] + state[c, j, pl.ds(r + 1, 8), :]
                av = (state[kap, j, rowset, :] + 4.0) * v - beside
                ex = jnp.exp(v)
                applied[c, j, rowset, :] = av
                intensity[c, j, rowset, :] = ex
                quad = v * av if quad is None else quad + v * av
                mass = ex if mass is None else mass + ex
            terms += [quad, mass]
        return terms

    def own_part():
        def body(i, sums):
            r = pl.multiple_of(TOP + i * 8, 8)
            return tuple(s + t for s, t in zip(sums, stencil_tiles(r, range(tiles))))

        zero = jnp.zeros((8, LANES), jnp.float32)
        return lax.fori_loop(0, rows // 8, body, (zero,) * (2 * chains))

    def halo_part():
        def side(i, carry):
            stencil_tiles(pl.multiple_of(TOP + i * 8, 8), [tiles])
            return carry

        def ends(i, carry):
            shift = jnp.where(i < HALO // 8, PAD, PAD + rows)
            stencil_tiles(pl.multiple_of(shift + i * 8, 8), range(tiles + 1))
            return carry

        lax.fori_loop(0, rows // 8, side, 0)
        lax.fori_loop(0, 2 * HALO // 8, ends, 0)

    def whole(x):
        return jnp.sum(jnp.sum(x, axis=0, keepdims=True), axis=1, keepdims=True)

    counted = whole(counted)

    def send(k, sums):
        q0, e0, q1, e1 = [whole(s) for s in sums]
        out = counted
        for i, value in enumerate((q0, q1, e0, e1)):
            out = jnp.where(seg[:1] == i, value, out)
        payload[k] = out
        gathered[k, me] = out
        for d in range(1, devices):
            pltpu.make_async_remote_copy(
                src_ref=payload.at[k], dst_ref=gathered.at[k, me],
                send_sem=sum_send.at[k], recv_sem=sum_recv.at[k],
                device_id=peer(d), device_id_type=MESH,
            ).start()

    def collect(k):
        bulk = gathered.at[k, pl.ds(0, devices - 1)]
        copy = pltpu.make_async_remote_copy(
            src_ref=bulk, dst_ref=bulk, send_sem=sum_send.at[k], recv_sem=sum_recv.at[k],
            device_id=peer(1), device_id_type=MESH,
        )
        copy.wait_recv()
        copy.wait_send()
        return jnp.broadcast_to(jnp.sum(gathered[k], axis=0), (8, LANES))

    def spread(values):
        out = jnp.zeros((8, LANES), jnp.float32)
        for i, value in enumerate(values):
            out = jnp.where(seg == i, value, out)
        return out

    h = [step_size[c] for c in range(chains)]
    hvec = spread([h[0], h[1], h[0], h[1]])
    hyp = spread([hyper[1, 0], hyper[1, 1], hyper[0, 0], hyper[0, 1]])
    vel = spread([velocity[1, 0], velocity[1, 1], velocity[0, 0], velocity[0, 1]])
    is_quad = seg < 2
    coef = jnp.where(is_quad, 0.5 / total, 1.0 / total)

    def accel(summed, expd):
        target = pltpu.roll(summed, LANES - 2 * SEG, 1) * (1.0 / total)
        return coef * expd * summed - jnp.where(is_quad, 0.5, target)

    def pick(x, i):
        return jnp.sum(jnp.where(lane == i * SEG, x, 0.0), axis=1, keepdims=True)

    def weights(expd, scale):
        scaled = expd * hvec * scale
        return [jnp.broadcast_to(pick(scaled, i), (8, LANES)) for i in range(2 * chains)]

    def kick(r, c, j, w, scale):
        rowset = pl.ds(r, 8)
        m = state[chains + c, j, rowset, :] + (h[c] * scale) * state[cnt, j, rowset, :]
        m = m - w[c] * applied[c, j, rowset, :] - w[chains + c] * intensity[c, j, rowset, :]
        state[chains + c, j, rowset, :] = m
        return m

    def advance(w, scale):
        def body(i, carry):
            r = pl.multiple_of(PAD + i * 8, 8)
            for c in range(chains):
                for j in range(tiles + 1):
                    m = kick(r, c, j, w, scale)
                    state[c, j, pl.ds(r, 8), :] += h[c] * m
            return carry

        lax.fori_loop(0, (rows + 2 * HALO) // 8, body, 0)

    def round_of(k):
        sums = own_part()
        send(k, sums)

    expd = jnp.exp(hyp)
    round_of(0)
    halo_part()
    advance(weights(expd, 0.5), 0.5)
    round_of(1)

    def step(k, carry):
        hyp, vel, expd = carry
        halo_part()
        a = accel(collect(k - 1), expd)
        vel = vel - jnp.where(k == 1, 0.5, 1.0) * hvec * a
        hyp = hyp + hvec * vel
        expd = jnp.exp(hyp)
        advance(weights(expd, 1.0), 1.0)
        round_of(k + 1)
        return hyp, vel, expd

    hyp, vel, expd = lax.fori_loop(1, STEPS, step, (hyp, vel, expd))

    def stores(base, out, start):
        copies = []
        for c in range(chains):
            for j in range(tiles):
                cols = pl.ds(j * LANES, LANES)
                copies.append(
                    pltpu.make_async_copy(
                        state.at[base + c, j, own, :],
                        out.at[c, :, cols],
                        store_sem.at[start + len(copies)],
                    )
                )
        for copy in copies:
            copy.start()
        return copies

    pending = stores(0, latent_out, 0)
    vel = vel - hvec * accel(collect(STEPS - 1), expd)
    hyp = hyp + hvec * vel
    expd = jnp.exp(hyp)
    w = weights(expd, 0.5)

    def final(i, carry):
        r = pl.multiple_of(TOP + i * 8, 8)
        for c in range(chains):
            for j in range(tiles):
                kick(r, c, j, w, 0.5)
        return carry

    lax.fori_loop(0, rows // 8, final, 0)
    pending += stores(chains, momentum_out, len(pending))
    vel = vel - 0.5 * hvec * accel(collect(STEPS), expd)

    out_row, out_col = sublane[:2, :2], lane[:2, :2]
    for x, ref in ((hyp, hyper_out), (vel, velocity_out)):
        picks = [pick(x, i)[:2] for i in range(2 * chains)]
        low = jnp.where(out_col == 0, picks[2], picks[3])
        high = jnp.where(out_col == 0, picks[0], picks[1])
        ref[...] = jnp.where(out_row == 0, low, high)
    for copy in pending:
        copy.wait()


def solution(mesh):
    nr, nc = mesh.shape["row"], mesh.shape["col"]
    devices = nr * nc

    def shards(latent, momentum, hyper_params, velocity, step_size, counts, kappa_field):
        chains, rows, cols = latent.shape
        tiles = cols // LANES
        deep = rows + 2 * TOP
        total = float(rows * nr * cols * nc)
        sizes = (nr, nc, chains, rows, tiles, total)
        anywhere = pl.BlockSpec(memory_space=pl.ANY)
        scalars = pl.BlockSpec(memory_space=pltpu.SMEM)
        small = pl.BlockSpec(memory_space=pltpu.VMEM)
        arrays = 2 * chains + 2
        f32 = jnp.float32
        return pl.pallas_call(
            functools.partial(kernel, sizes),
            out_shape=(
                jax.ShapeDtypeStruct(latent.shape, f32),
                jax.ShapeDtypeStruct(latent.shape, f32),
                jax.ShapeDtypeStruct(hyper_params.shape, f32),
                jax.ShapeDtypeStruct(velocity.shape, f32),
            ),
            in_specs=[anywhere] * 4 + [scalars] * 3,
            out_specs=(anywhere, anywhere, small, small),
            scratch_shapes=[
                pltpu.VMEM((arrays, tiles + 1, deep, LANES), f32),
                pltpu.VMEM((chains, tiles + 1, deep, LANES), f32),
                pltpu.VMEM((chains, tiles + 1, deep, LANES), f32),
                pltpu.VMEM((tiles, rows, LANES), jnp.int32),
                pltpu.VMEM((rows, LANES), f32),
                pltpu.VMEM((rows, LANES), f32),
                pltpu.VMEM((rows + 2 * HALO, LANES), f32),
                pltpu.VMEM((rows + 2 * HALO, LANES), f32),
                pltpu.VMEM((STEPS + 1, 1, LANES), f32),
                pltpu.VMEM((STEPS + 1, devices, 1, LANES), f32),
                pltpu.SemaphoreType.DMA((2 * tiles * (chains + 1),)),
                pltpu.SemaphoreType.DMA((2 * tiles * chains,)),
                pltpu.SemaphoreType.DMA((8,)),
                pltpu.SemaphoreType.DMA((8,)),
                pltpu.SemaphoreType.DMA((STEPS + 1,)),
                pltpu.SemaphoreType.DMA((STEPS + 1,)),
            ],
            compiler_params=pltpu.CompilerParams(collective_id=0, has_side_effects=True),
        )(latent, momentum, counts, kappa_field, hyper_params, velocity, step_size)

    placed = (
        P(None, "row", "col"),
        P(None, "row", "col"),
        P(),
        P(),
        P(),
        P("row", "col"),
        P("row", "col"),
    )
    return jax.shard_map(
        shards,
        mesh=mesh,
        in_specs=placed,
        out_specs=(P(None, "row", "col"), P(None, "row", "col"), P(), P()),
        check_vma=False,
    )
```

time: 557 us -> 95.3 us (0.17)
  blocking collectives: 438 us -> 0 us
  Pallas kernels: 0 us -> 90.5 us
  other arithmetic: 47.7 us -> 0 us
  waiting for transfers between devices: 35.5 us -> 0 us
  starting transfers between devices: 25.7 us -> 0 us
    psum x11 -> x0, blocking collectives: 438 us -> none  [acceleration(): summed = lax.psum(stacked, ('row', 'col'))]
    pallas_call x0 -> x1, Pallas kernels: none -> 90.5 us  [shards(): pl.pallas_call(functools.partial(kernel, sizes), out_shape=(jax.ShapeDtyp...]
    ppermute x24 -> x0, waiting for transfers between devices: 35.5 us -> none  [the longest x12 26.8 us: padded(): lax.ppermute(tail, axis, [(i, (i + 1) % count) for i in range(count)])]
    add x26 -> x0, other arithmetic: 32.3 us -> none  [the longest x10 29 us: shards(): field = field + size_grid * moment]
    ppermute x24 -> x0, starting transfers between devices: 25.7 us -> none  [the longest x12 22.6 us: padded(): lax.ppermute(head, axis, [((i + 1) % count, i) for i in range(count)])]
    reduce_sum x19 -> x0, other arithmetic: 8.7 us -> none  [the longest x10 5.69 us: local_gradient(): jnp.sum(weighted, axis=(1, 2))]
    slice x17 -> x0, local copies, waits for them, and re-layouts: 6.15 us -> none  [the longest x4 3.7 us: trimmed(): return array[..., layers:-layers, layers:-layers]]
  transfers between devices with their start and end apart: 24 -> 0, of which waited for: 17 -> 0; matrix products, arithmetic and copies ran while one was open for 2% -> 0% of each run, Pallas kernels for 0% -> 0%
where the time goes in v1:
time: 95.3 us; the launch traced here: 95.1 us
  Pallas kernels  90.5 us (95%)
  local copies, waits for them, and re-layouts  3.95 us (4%)
    pallas_call x1, Pallas kernels, shards(): pl.pallas_call(functools.partial(kernel, sizes), out_shape=(jax.ShapeDtyp...  90.5 us
    unnamed x10, local copies, waits for them, and re-layouts  3.95 us

profile of v1, /device:TPU:0, one launch (start us, length us, event | category | flops | bytes accessed | tf_op | source)
XLA Modules:
  0.0 95.1 jit_solution(4043970959863633519)
XLA Ops:
  0.6 90.5 %shard_map.102 = (f32[2,256,256]{2,1,0:T(8,128)}, f32[2,256,256]{2,1,0:T(8,128)}, f32[2,2]{1,0:T(2,128)}, f32[2,2]{1,0:T(2,128)}) custom-call(f32[2,256,256]{2,1,0:T(8,128)} %latent.1, f32[2,256,256]{2,1,0:T(8,128)} %momentum.1, s32[256,256]{1,0:T(8,128)} %counts.1, f32[256,256]{1,0:T(8,128)} %kappa.1, f32[2,2]{1,0:T(2,128)} %hyper.1, f32[2,2]{1,0:T(2,128)} %velocity.1, ...), custom_call_target="tpu_custom_call" | custom-call | tf_op jit(solution)/shard_map/pallas_call | solution.py:328
  91.1 0.0 copy-start
  91.1 1.9 %copy.15 = f32[2,256,256]{2,1,0:T(8,128)} copy(f32[2,256,256]{2,1,0:T(8,128)} %get-tuple-element.8) | data formatting | bytes 1048576
  93.0 0.0 copy-done
  93.0 0.0 copy-start.2
  93.1 0.8 copy.16
  93.8 0.0 copy-done.2
  93.8 0.0 copy-start.1
  93.9 0.6 copy.17
  94.4 0.1 copy-done.1
  94.5 0.6 copy.18
Async XLA Ops:
  91.1 1.9 %copy-start = (f32[2,256,256]{2,1,0:T(8,128)S(1)}, f32[2,256,256]{2,1,0:T(8,128)}, u32[]{:S(2)}) copy-start(f32[2,256,256]{2,1,0:T(8,128)} %get-tuple-element.9) | copy-start | bytes 1572868
  93.0 0.8 copy-start.2
  93.8 0.7 copy-start.1

commit v2 on v1

--- a/solution.py
+++ b/solution.py
@@ -12,6 +12,7 @@
 PAD = 8
 TOP = PAD + HALO
 LANES = 128
+OWN_DEEP, SIDE_DEEP, KICK_DEEP, PACK_DEEP, UNPACK_DEEP = 128, 128, 32, 64, 96
 SEG = 16
 MESH = pl.DeviceIdType.MESH
 
@@ -19,7 +20,7 @@
 def kernel(
     sizes, latent, momentum, counts, kappa, hyper, velocity, step_size,
     latent_out, momentum_out, hyper_out, velocity_out,
-    state, applied, intensity, raw_counts, left_pack, right_pack, from_right, from_left,
+    state, diagonal, applied, intensity, raw_counts, left_pack, right_pack, from_right, from_left,
     payload, gathered,
     load_sem, store_sem, halo_send, halo_recv, sum_send, sum_recv,
 ):
@@ -56,29 +57,31 @@
     lane = lax.broadcasted_iota(jnp.int32, (8, LANES), 1)
     seg = lane // SEG
     sublane = lax.broadcasted_iota(jnp.int32, (8, LANES), 0)
-    first, last = lane == 0, lane == LANES - 1
+    first = lax.broadcasted_iota(jnp.int32, (1, LANES), 1) == 0
+    last = lax.broadcasted_iota(jnp.int32, (1, LANES), 1) == LANES - 1
 
     for copy in loads:
         copy.wait()
 
     def pack(i, counted):
-        rel = pl.multiple_of(i * 8, 8)
-        r = pl.multiple_of(TOP + i * 8, 8)
+        rel = pl.ds(pl.multiple_of(i * PACK_DEEP, 8), PACK_DEEP)
+        here = pl.ds(pl.multiple_of(TOP + i * PACK_DEEP, 8), PACK_DEEP)
+        value = [raw_counts[j, rel, :].astype(jnp.float32) for j in range(tiles)]
+        heads = [state[a, 0, here, :] for a in range(arrays - 1)] + [value[0]]
+        tails = [state[a, tiles - 1, here, :] for a in range(arrays - 1)] + [value[-1]]
+        lp, rp = heads[0], pltpu.roll(tails[0], SEG, 1)
+        for a in range(1, arrays):
+            lp = jnp.where(seg[:1] == a, pltpu.roll(heads[a], SEG * a, 1), lp)
+            rp = jnp.where(seg[:1] == a, pltpu.roll(tails[a], SEG * (a + 1) % LANES, 1), rp)
+        left_pack[rel, :] = lp
+        right_pack[rel, :] = rp
         for j in range(tiles):
-            value = raw_counts[j, pl.ds(rel, 8), :].astype(jnp.float32)
-            state[cnt, j, pl.ds(r, 8), :] = value
-            counted = counted + value
-        lp = state[0, 0, pl.ds(r, 8), :]
-        rp = pltpu.roll(state[0, tiles - 1, pl.ds(r, 8), :], SEG, 1)
-        for a in range(1, arrays):
-            lp = jnp.where(seg == a, pltpu.roll(state[a, 0, pl.ds(r, 8), :], SEG * a, 1), lp)
-            rolled = pltpu.roll(state[a, tiles - 1, pl.ds(r, 8), :], SEG * (a + 1) % LANES, 1)
-            rp = jnp.where(seg == a, rolled, rp)
-        left_pack[pl.ds(rel, 8), :] = lp
-        right_pack[pl.ds(rel, 8), :] = rp
-        return counted
-
-    counted = lax.fori_loop(0, rows // 8, pack, jnp.zeros((8, LANES), jnp.float32))
+            state[cnt, j, here, :] = value[j]
+        both = sum(value)
+        return counted + sum(both[8 * u : 8 * u + 8] for u in range(PACK_DEEP // 8))
+
+    zeros = jnp.zeros((8, LANES), jnp.float32)
+    counted = lax.fori_loop(0, rows // PACK_DEEP, pack, zeros)
 
     pl.semaphore_wait(barrier, devices - 1)
 
@@ -117,61 +120,67 @@
         copy.wait()
 
     def unpack(i, carry):
-        rel = pl.multiple_of(i * 8, 8)
-        r = pl.multiple_of(PAD + i * 8, 8)
-        fr = from_right[pl.ds(rel, 8), :]
-        fl = from_left[pl.ds(rel, 8), :]
+        rel = pl.ds(pl.multiple_of(i * UNPACK_DEEP, 8), UNPACK_DEEP)
+        here = pl.ds(pl.multiple_of(PAD + i * UNPACK_DEEP, 8), UNPACK_DEEP)
+        fr, fl = from_right[rel, :], from_left[rel, :]
+        values = []
         for a in range(arrays):
-            right_part = pltpu.roll(fr, (LANES - SEG * a) % LANES, 1)
+            right_part = pltpu.roll(fr, (LANES - SEG * a) % LANES, 1) if a else fr
             left_part = pltpu.roll(fl, (LANES - SEG * (a + 1)) % LANES, 1)
-            value = jnp.where(seg == 0, right_part, jnp.where(seg == 7, left_part, 0.0))
-            state[a, tiles, pl.ds(r, 8), :] = value
+            left_part = jnp.where(seg[:1] == 7, left_part, 0.0)
+            values.append(jnp.where(seg[:1] == 0, right_part, left_part))
+        plus = [state[kap, j, here, :] + 4.0 for j in range(tiles)] + [values[kap] + 4.0]
+        for a in range(arrays):
+            state[a, tiles, here, :] = values[a]
+        for j in range(tiles + 1):
+            diagonal[j, here, :] = plus[j]
         return carry
 
-    lax.fori_loop(0, (rows + 2 * HALO) // 8, unpack, 0)
-
-    def stencil_tiles(r, lane_tiles):
-        rowset = pl.ds(r, 8)
-        terms = []
+    lax.fori_loop(0, (rows + 2 * HALO) // UNPACK_DEEP, unpack, 0)
+
+    def stencil_tiles(r, deep, lane_tiles):
+        rowset = pl.ds(r, deep)
+        terms, results = [], []
         for c in range(chains):
             full = [state[c, j, rowset, :] for j in range(tiles + 1)]
-            to_right = [pltpu.roll(x, 1, 1) for x in full]
-            to_left = [pltpu.roll(x, LANES - 1, 1) for x in full]
+            used = sorted({(j + s) % (tiles + 1) for j in lane_tiles for s in (-1, 0)})
+            to_right = {j: pltpu.roll(full[j], 1, 1) for j in used}
+            used = sorted({(j + s) % (tiles + 1) for j in lane_tiles for s in (1, 0)})
+            to_left = {j: pltpu.roll(full[j], LANES - 1, 1) for j in used}
             quad = mass = None
             for j in lane_tiles:
                 v = full[j]
-                beside = jnp.where(first, to_right[j - 1], to_right[j])
+                beside = jnp.where(first, to_right[(j - 1) % (tiles + 1)], to_right[j])
                 beside += jnp.where(last, to_left[(j + 1) % (tiles + 1)], to_left[j])
-                beside += state[c, j, pl.ds(r - 1, 8), :] + state[c, j, pl.ds(r + 1, 8), :]
-                av = (state[kap, j, rowset, :] + 4.0) * v - beside
+                beside += state[c, j, pl.ds(r - 1, deep), :] + state[c, j, pl.ds(r + 1, deep), :]
+                av = diagonal[j, rowset, :] * v - beside
                 ex = jnp.exp(v)
-                applied[c, j, rowset, :] = av
-                intensity[c, j, rowset, :] = ex
+                results.append((c, j, av, ex))
                 quad = v * av if quad is None else quad + v * av
                 mass = ex if mass is None else mass + ex
             terms += [quad, mass]
-        return terms
+        for c, j, av, ex in results:
+            applied[c, j, rowset, :] = av
+            intensity[c, j, rowset, :] = ex
+        return [sum(t[8 * u : 8 * u + 8] for u in range(deep // 8)) for t in terms]
 
     def own_part():
         def body(i, sums):
-            r = pl.multiple_of(TOP + i * 8, 8)
-            return tuple(s + t for s, t in zip(sums, stencil_tiles(r, range(tiles))))
+            r = pl.multiple_of(TOP + i * OWN_DEEP, 8)
+            terms = stencil_tiles(r, OWN_DEEP, range(tiles))
+            return tuple(s + t for s, t in zip(sums, terms))
 
         zero = jnp.zeros((8, LANES), jnp.float32)
-        return lax.fori_loop(0, rows // 8, body, (zero,) * (2 * chains))
+        return lax.fori_loop(0, rows // OWN_DEEP, body, (zero,) * (2 * chains))
 
     def halo_part():
         def side(i, carry):
-            stencil_tiles(pl.multiple_of(TOP + i * 8, 8), [tiles])
+            stencil_tiles(pl.multiple_of(TOP + i * SIDE_DEEP, 8), SIDE_DEEP, [tiles])
             return carry
 
-        def ends(i, carry):
-            shift = jnp.where(i < HALO // 8, PAD, PAD + rows)
-            stencil_tiles(pl.multiple_of(shift + i * 8, 8), range(tiles + 1))
-            return carry
-
-        lax.fori_loop(0, rows // 8, side, 0)
-        lax.fori_loop(0, 2 * HALO // 8, ends, 0)
+        lax.fori_loop(0, rows // SIDE_DEEP, side, 0)
+        stencil_tiles(PAD, HALO, range(tiles + 1))
+        stencil_tiles(TOP + rows, HALO, range(tiles + 1))
 
     def whole(x):
         return jnp.sum(jnp.sum(x, axis=0, keepdims=True), axis=1, keepdims=True)
@@ -224,25 +233,27 @@
 
     def weights(expd, scale):
         scaled = expd * hvec * scale
-        return [jnp.broadcast_to(pick(scaled, i), (8, LANES)) for i in range(2 * chains)]
-
-    def kick(r, c, j, w, scale):
-        rowset = pl.ds(r, 8)
+        return [jnp.broadcast_to(pick(scaled, i)[:1], (1, LANES)) for i in range(2 * chains)]
+
+    def kick(r, deep, c, j, w, scale):
+        rowset = pl.ds(r, deep)
         m = state[chains + c, j, rowset, :] + (h[c] * scale) * state[cnt, j, rowset, :]
-        m = m - w[c] * applied[c, j, rowset, :] - w[chains + c] * intensity[c, j, rowset, :]
-        state[chains + c, j, rowset, :] = m
-        return m
+        return m - w[c] * applied[c, j, rowset, :] - w[chains + c] * intensity[c, j, rowset, :]
 
     def advance(w, scale):
         def body(i, carry):
-            r = pl.multiple_of(PAD + i * 8, 8)
+            rowset = pl.ds(pl.multiple_of(PAD + i * KICK_DEEP, 8), KICK_DEEP)
+            moved = []
             for c in range(chains):
                 for j in range(tiles + 1):
-                    m = kick(r, c, j, w, scale)
-                    state[c, j, pl.ds(r, 8), :] += h[c] * m
+                    m = kick(rowset.start, KICK_DEEP, c, j, w, scale)
+                    moved.append((c, j, m, state[c, j, rowset, :] + h[c] * m))
+            for c, j, m, v in moved:
+                state[chains + c, j, rowset, :] = m
+                state[c, j, rowset, :] = v
             return carry
 
-        lax.fori_loop(0, (rows + 2 * HALO) // 8, body, 0)
+        lax.fori_loop(0, (rows + 2 * HALO) // KICK_DEEP, body, 0)
 
     def round_of(k):
         sums = own_part()
@@ -290,13 +301,16 @@
     w = weights(expd, 0.5)
 
     def final(i, carry):
-        r = pl.multiple_of(TOP + i * 8, 8)
+        rowset = pl.ds(pl.multiple_of(TOP + i * KICK_DEEP, 8), KICK_DEEP)
+        moved = []
         for c in range(chains):
             for j in range(tiles):
-                kick(r, c, j, w, 0.5)
+                moved.append((c, j, kick(rowset.start, KICK_DEEP, c, j, w, 0.5)))
+        for c, j, m in moved:
+            state[chains + c, j, rowset, :] = m
         return carry
 
-    lax.fori_loop(0, rows // 8, final, 0)
+    lax.fori_loop(0, rows // KICK_DEEP, final, 0)
     pending += stores(chains, momentum_out, len(pending))
     vel = vel - 0.5 * hvec * accel(collect(STEPS), expd)
 
@@ -337,6 +351,7 @@
             out_specs=(anywhere, anywhere, small, small),
             scratch_shapes=[
                 pltpu.VMEM((arrays, tiles + 1, deep, LANES), f32),
+                pltpu.VMEM((tiles + 1, deep, LANES), f32),
                 pltpu.VMEM((chains, tiles + 1, deep, LANES), f32),
                 pltpu.VMEM((chains, tiles + 1, deep, LANES), f32),
                 pltpu.VMEM((tiles, rows, LANES), jnp.int32),

time: 95.3 us -> 54.5 us (0.57)
  Pallas kernels: 90.5 us -> 49.7 us
    pallas_call x1, Pallas kernels: 90.5 us -> 49.7 us  [shards(): pl.pallas_call(functools.partial(kernel, sizes), out_shape=(jax.ShapeDtyp...]
where the time goes in v2:
time: 54.5 us; the launch traced here: 54.3 us
  Pallas kernels  49.7 us (91%)
  local copies, waits for them, and re-layouts  3.95 us (7%)
  between operations  0.65 us (1%)
    pallas_call x1, Pallas kernels, shards(): pl.pallas_call(functools.partial(kernel, sizes), out_shape=(jax.ShapeDtyp...  49.7 us
    unnamed x10, local copies, waits for them, and re-layouts  3.95 us

profile of v2, /device:TPU:0, one launch (start us, length us, event | category | flops | bytes accessed | tf_op | source)
XLA Modules:
  0.0 54.3 jit_solution(13906886863882387904)
XLA Ops:
  0.6 49.7 %shard_map.102 = (f32[2,256,256]{2,1,0:T(8,128)}, f32[2,256,256]{2,1,0:T(8,128)}, f32[2,2]{1,0:T(2,128)}, f32[2,2]{1,0:T(2,128)}) custom-call(f32[2,256,256]{2,1,0:T(8,128)} %latent.1, f32[2,256,256]{2,1,0:T(8,128)} %momentum.1, s32[256,256]{1,0:T(8,128)} %counts.1, f32[256,256]{1,0:T(8,128)} %kappa.1, f32[2,2]{1,0:T(2,128)} %hyper.1, f32[2,2]{1,0:T(2,128)} %velocity.1, ...), custom_call_target="tpu_custom_call" | custom-call | tf_op jit(solution)/shard_map/pallas_call | solution.py:342
  50.4 0.0 copy-start
  50.4 1.9 %copy.15 = f32[2,256,256]{2,1,0:T(8,128)} copy(f32[2,256,256]{2,1,0:T(8,128)} %get-tuple-element.8) | data formatting | bytes 1048576
  52.3 0.0 copy-done
  52.3 0.0 copy-start.2
  52.3 0.8 %copy.16 = f32[2,256,256]{2,1,0:T(8,128)} copy(f32[2,256,256]{2,1,0:T(8,128)S(1)} %copy-done) | data formatting | bytes 1048576
  53.1 0.0 copy-done.2
  53.1 0.0 copy-start.1
  53.1 0.6 %copy.17 = f32[2,2]{1,0:T(2,128)} copy(f32[2,2]{1,0:T(2,128)S(1)} %copy-done.2) | data formatting | bytes 32
  53.7 0.1 copy-done.1
  53.8 0.6 %copy.18 = f32[2,2]{1,0:T(2,128)} copy(f32[2,2]{1,0:T(2,128)S(1)} %copy-done.1) | data formatting | bytes 32
Async XLA Ops:
  50.4 1.9 %copy-start = (f32[2,256,256]{2,1,0:T(8,128)S(1)}, f32[2,256,256]{2,1,0:T(8,128)}, u32[]{:S(2)}) copy-start(f32[2,256,256]{2,1,0:T(8,128)} %get-tuple-element.9) | copy-start | bytes 1572868
  52.3 0.8 %copy-start.2 = (f32[2,2]{1,0:T(2,128)S(1)}, f32[2,2]{1,0:T(2,128)}, u32[]{:S(2)}) copy-start(f32[2,2]{1,0:T(2,128)} %get-tuple-element.10) | copy-start | bytes 52
  53.1 0.7 %copy-start.1 = (f32[2,2]{1,0:T(2,128)S(1)}, f32[2,2]{1,0:T(2,128)}, u32[]{:S(2)}) copy-start(f32[2,2]{1,0:T(2,128)} %get-tuple-element.11) | copy-start | bytes 52

commit v3 on v2

--- a/solution.py
+++ b/solution.py
@@ -12,7 +12,7 @@
 PAD = 8
 TOP = PAD + HALO
 LANES = 128
-OWN_DEEP, SIDE_DEEP, KICK_DEEP, PACK_DEEP, UNPACK_DEEP = 128, 128, 32, 64, 96
+OWN_DEEP, SIDE_DEEP, KICK_DEEP, PACK_DEEP, UNPACK_DEEP = 256, 256, 48, 64, 96
 SEG = 16
 MESH = pl.DeviceIdType.MESH
 
@@ -51,7 +51,7 @@
         return (other // nc, lax.rem(other, nc))
 
     barrier = pltpu.get_barrier_semaphore()
-    for d in range(1, devices):
+    for d in sorted(range(1, devices), key=lambda d: -min(d, devices - d)):
         pl.semaphore_signal(barrier, inc=1, device_id=peer(d), device_id_type=MESH)
 
     lane = lax.broadcasted_iota(jnp.int32, (8, LANES), 1)
@@ -194,7 +194,7 @@
             out = jnp.where(seg[:1] == i, value, out)
         payload[k] = out
         gathered[k, me] = out
-        for d in range(1, devices):
+        for d in sorted(range(1, devices), key=lambda d: -min(d, devices - d)):
             pltpu.make_async_remote_copy(
                 src_ref=payload.at[k], dst_ref=gathered.at[k, me],
                 send_sem=sum_send.at[k], recv_sem=sum_recv.at[k],
@@ -208,7 +208,6 @@
             device_id=peer(1), device_id_type=MESH,
         )
         copy.wait_recv()
-        copy.wait_send()
         return jnp.broadcast_to(jnp.sum(gathered[k], axis=0), (8, LANES))
 
     def spread(values):
@@ -301,16 +300,16 @@
     w = weights(expd, 0.5)
 
     def final(i, carry):
-        rowset = pl.ds(pl.multiple_of(TOP + i * KICK_DEEP, 8), KICK_DEEP)
+        rowset = pl.ds(pl.multiple_of(TOP + i * PACK_DEEP, 8), PACK_DEEP)
         moved = []
         for c in range(chains):
             for j in range(tiles):
-                moved.append((c, j, kick(rowset.start, KICK_DEEP, c, j, w, 0.5)))
+                moved.append((c, j, kick(rowset.start, PACK_DEEP, c, j, w, 0.5)))
         for c, j, m in moved:
             state[chains + c, j, rowset, :] = m
         return carry
 
-    lax.fori_loop(0, rows // KICK_DEEP, final, 0)
+    lax.fori_loop(0, rows // PACK_DEEP, final, 0)
     pending += stores(chains, momentum_out, len(pending))
     vel = vel - 0.5 * hvec * accel(collect(STEPS), expd)
 
@@ -321,6 +320,29 @@
         high = jnp.where(out_col == 0, picks[0], picks[1])
         ref[...] = jnp.where(out_row == 0, low, high)
     for copy in pending:
+        copy.wait()
+
+    def drain(k, carry):
+        bulk = gathered.at[k, pl.ds(0, devices - 1)]
+        pltpu.make_async_remote_copy(
+            src_ref=bulk, dst_ref=bulk, send_sem=sum_send.at[k], recv_sem=sum_recv.at[k],
+            device_id=peer(1), device_id_type=MESH,
+        ).wait_send()
+        return carry
+
+    lax.fori_loop(0, STEPS + 1, drain, 0)
+
+
+def hand_out(latent, momentum, hyper, velocity, latent_out, momentum_out, hyper_out, velocity_out, sems):
+    copies = [
+        pltpu.make_async_copy(latent, latent_out, sems.at[0]),
+        pltpu.make_async_copy(momentum, momentum_out, sems.at[1]),
+    ]
+    for copy in copies:
+        copy.start()
+    hyper_out[...] = hyper[...]
+    velocity_out[...] = velocity[...]
+    for copy in copies:
         copy.wait()
 
 
@@ -339,7 +361,7 @@
         small = pl.BlockSpec(memory_space=pltpu.VMEM)
         arrays = 2 * chains + 2
         f32 = jnp.float32
-        return pl.pallas_call(
+        results = pl.pallas_call(
             functools.partial(kernel, sizes),
             out_shape=(
                 jax.ShapeDtypeStruct(latent.shape, f32),
@@ -370,6 +392,13 @@
             ],
             compiler_params=pltpu.CompilerParams(collective_id=0, has_side_effects=True),
         )(latent, momentum, counts, kappa_field, hyper_params, velocity, step_size)
+        return pl.pallas_call(
+            hand_out,
+            out_shape=[jax.ShapeDtypeStruct(x.shape, f32) for x in results],
+            in_specs=[small] * 4,
+            out_specs=[anywhere] * 2 + [small] * 2,
+            scratch_shapes=[pltpu.SemaphoreType.DMA((2,))],
+        )(*results)
 
     placed = (
         P(None, "row", "col"),

time: 54.5 us -> 53.2 us (0.976)
  local copies, waits for them, and re-layouts: 3.95 us -> 0 us
  Pallas kernels: 49.7 us -> 52.4 us
    unnamed x10 -> x0, local copies, waits for them, and re-layouts: 3.95 us -> none
    pallas_call x0 -> x1, Pallas kernels: none -> 2.75 us  [shards(): pl.pallas_call(hand_out, out_shape=[jax.ShapeDtypeStruct(x.shape, f32) fo...]
where the time goes in v3:
time: 53.2 us; the launch traced here: 53 us
  Pallas kernels  52.4 us (98%)
  between operations  0.64 us (1%)
    pallas_call x1, Pallas kernels, shards(): pl.pallas_call(functools.partial(kernel, sizes), out_shape=(jax.ShapeDtyp...  49.7 us
    pallas_call x1, Pallas kernels, shards(): pl.pallas_call(hand_out, out_shape=[jax.ShapeDtypeStruct(x.shape, f32) fo...  2.75 us

profile of v3, /device:TPU:0, one launch (start us, length us, event | category | flops | bytes accessed | tf_op | source)
XLA Modules:
  0.0 53.0 jit_solution(4283854074637501799)
XLA Ops:
  0.6 49.7 %shard_map.102 = (f32[2,256,256]{2,1,0:T(8,128)}, f32[2,256,256]{2,1,0:T(8,128)}, f32[2,2]{1,0:T(2,128)}, f32[2,2]{1,0:T(2,128)}) custom-call(f32[2,256,256]{2,1,0:T(8,128)} %latent.1, f32[2,256,256]{2,1,0:T(8,128)} %momentum.1, s32[256,256]{1,0:T(8,128)} %counts.1, f32[256,256]{1,0:T(8,128)} %kappa.1, f32[2,2]{1,0:T(2,128)} %hyper.1, f32[2,2]{1,0:T(2,128)} %velocity.1, ...), custom_call_target="tpu_custom_call" | custom-call | tf_op jit(solution)/shard_map/pallas_call | solution.py:364
  50.3 2.8 %shard_map.103 = (f32[2,256,256]{2,1,0:T(8,128)}, f32[2,256,256]{2,1,0:T(8,128)}, f32[2,2]{1,0:T(2,128)}, f32[2,2]{1,0:T(2,128)}) custom-call(f32[2,256,256]{2,1,0:T(8,128)} %get-tuple-element.8.latent, f32[2,256,256]{2,1,0:T(8,128)} %get-tuple-element.9.momentum, f32[2,2]{1,0:T(2,128)} %get-tuple-element.10.hyper, f32[2,2]{1,0:T(2,128)} %get-tuple-element.11.velocity), custom_call_target="tpu_custom_call" | custom-call | tf_op jit(solution)/shard_map/pallas_call | solution.py:395
